TPU v7x, 32 devices: a whole 2x2x4 slice. The times are simulated.
32 devices in a mesh: batch: 2 (over x), row: 4 (over z), col: 4 (over y, core).
Axes of the slice: x: 2, y: 2, z: 4, core: 2. Of those that a mesh axis runs over, the one named last changes fastest.
Arguments:
- a_mat: bfloat16 [6144, 32768], P(('batch', 'row'), 'col'), parts along dimension 0
Outputs:
- output: bfloat16 [6144, 3072], P(('batch', 'row'), 'col'), parts along dimension 0
There are 2 independent parts. A program takes and returns all parts, laid end to end along the dimension named above; each array names one.
All inputs are finite; a program needn't handle non-finite values.
Results may differ from a plain program's by a relative error of at most 0.001.
Values are sent between devices in bfloat16 or wider.
A program may use at most 1 GiB of HBM per device.

v0:
```python
import jax
import jax.numpy as jnp
from jax import lax
from jax.sharding import PartitionSpec as P

BLOCK = 256


def lower_part(row_panel, col_panel, row_step, row_pos, col_step, col_pos):
    row_blocks = row_panel.shape[0] // BLOCK
    col_blocks = col_panel.shape[0] // BLOCK
    col_total = col_panel.shape[0]
    band_size = max(1, row_blocks // 8)
    col_local = jnp.arange(col_total)
    col_index = ((col_local // BLOCK) * col_step + col_pos) * BLOCK + col_local % BLOCK
    pieces = []
    for first_blk in range(0, row_blocks, band_size):
        last_blk = min(first_blk + band_size, row_blocks)
        col_width = BLOCK * min(col_blocks, (last_blk * row_step - 1) // col_step + 1)
        product = lax.dot_general(row_panel[first_blk * BLOCK:last_blk * BLOCK], col_panel[:col_width], (((1,), (1,)), ((), ())), preferred_element_type=jnp.float32)
        row_local = jnp.arange(first_blk * BLOCK, last_blk * BLOCK)
        row_index = ((row_local // BLOCK) * row_step + row_pos) * BLOCK + row_local % BLOCK
        kept_vals = jnp.where(row_index[:, None] >= col_index[None, :col_width], product, 0.0).astype(jnp.bfloat16)
        pieces.append(jnp.pad(kept_vals, ((0, 0), (0, col_total - col_width))))
    return jnp.concatenate(pieces, axis=0)


def solution(mesh):
    row_count = mesh.shape['row']
    col_count = mesh.shape['col']

    def local_fn(a_local):
        local_rows, m_local = a_local.shape
        n_total = local_rows * row_count
        row_pos = lax.axis_index('row')
        col_pos = lax.axis_index('col')
        row_panel = lax.all_gather(a_local, 'col', axis=1, tiled=True)
        gathered = lax.all_gather(a_local.reshape(local_rows // BLOCK, BLOCK, m_local), 'row', axis=1)
        grouped = gathered.reshape(n_total // (BLOCK * col_count), col_count, BLOCK, m_local)
        swapped = lax.all_to_all(grouped, 'col', 1, 3, tiled=True)
        col_panel = swapped.reshape(n_total // col_count, m_local * col_count)
        return lower_part(row_panel, col_panel, row_count, row_pos, col_count, col_pos)

    part_spec = P(('batch', 'row'), 'col')
    return jax.shard_map(local_fn, mesh=mesh, in_specs=(part_spec,), out_specs=part_spec, check_vma=False)
```

profile of v0, /device:TPU:8, one launch (start us, length us, event | category | flops | bytes accessed | tf_op | source)
XLA Modules:
  0.0 2024.1 jit_solution(1208673410859681960)
XLA Ops:
  6.5 0.0 all-gather.5.cloned.1.call-start
  6.5 0.7 all-gather.5.cloned.1.call-update
  7.3 0.0 all-gather.3.cloned.1.call-start
  7.3 0.7 all-gather.3.cloned.1.call-update
  8.0 836.3 %all-gather.5.cloned.1.call-done = bf16[3,4,256,8192]{3,2,0,1:T(8,128)(2,1)} async-done(((bf16[3,1,256,8192]{3,2,0,1:T(8,128)(2,1)}), bf16[3,4,256,8192]{3,2,0,1:T(8,128)(2,1)}) %all-gather.5.cloned.1.call-update) | async-done | bytes 50331664 | tf_op jit(solution)/shard_map/all_gather | solution.py:38
  844.3 64.5 %copy.10 = bf16[3,4,256,8192]{2,3,0,1:T(8,128)(2,1)} copy(bf16[3,4,256,8192]{3,2,0,1:T(8,128)(2,1)} %all-gather.5.cloned.1.call-done) | data formatting | bytes 100663296 | tf_op jit(solution)/shard_map/all_gather | solution.py:38
  908.8 11.7 all-to-all-start
  920.6 0.0 copy-start
  920.6 0.6 copy-done
  921.1 0.6 fusion.44
  921.7 0.6 fusion.42
  922.3 757.7 %all-to-all-done = bf16[3,4,256,8192]{2,3,0,1:T(8,128)(2,1)} async-done(((bf16[3,4,256,8192]{2,3,0,1:T(8,128)(2,1)}), bf16[3,4,256,8192]{2,3,0,1:T(8,128)(2,1)}, u32[]{:S(2)}, u32[]{:S(2)}) %all-to-all-start) | async-done | bytes 50331680 | tf_op jit(solution)/shard_map/all_to_all | solution.py:40
  1680.1 33.4 %copy.17 = bf16[3,4,256,8192]{2,3,1,0:T(8,128)(2,1)} copy(bf16[3,4,256,8192]{2,3,0,1:T(8,128)(2,1)} %all-to-all-done) | data formatting | bytes 100663296 | tf_op jit(solution)/shard_map/all_to_all | solution.py:40
  1713.5 22.9 %slice.39 = bf16[2,1,256,4,8192]{2,4,3,1,0:T(8,128)(2,1)} slice(bf16[3,1,256,4,8192]{2,4,3,1,0:T(8,128)(2,1)} %bitcast.18), slice={[0:2], [0:1], [0:256], [0:4], [0:8192]} | slice | bytes 67108864 | tf_op jit(solution)/shard_map/slice | solution.py:20
  1736.4 13.7 slice.37
  1750.1 81.9 %copy.13 = bf16[3,1,256,4,8192]{4,3,2,0,1:T(4,128)(2,1)} copy(bf16[3,1,256,4,8192]{2,4,3,1,0:T(8,128)(2,1)} %bitcast.20) | data formatting | bytes 100663296 | tf_op jit(solution)/shard_map/all_to_all | solution.py:40
  1832.0 54.9 %copy.12 = bf16[2,1,256,4,8192]{4,3,2,0,1:T(4,128)(2,1)} copy(bf16[2,1,256,4,8192]{2,4,3,1,0:T(8,128)(2,1)} %slice.39) | data formatting | bytes 67108864 | tf_op jit(solution)/shard_map/slice | solution.py:20
  1886.9 29.2 %copy.14 = bf16[64,8,4,8192]{3,1,2,0:T(8,128)(2,1)} copy(bf16[64,8,4,8192]{3,2,1,0:T(4,128)(2,1)} %bitcast.22) | data formatting | bytes 67108864
  1916.1 0.0 copy-start.1
  1916.1 0.0 copy-start.4
  1916.1 42.3 %copy.15 = bf16[96,8,4,8192]{3,1,2,0:T(8,128)(2,1)} copy(bf16[96,8,4,8192]{3,2,1,0:T(4,128)(2,1)} %bitcast.21) | data formatting | bytes 100663296
  1958.5 0.0 all-gather.3.cloned.1.call-done
  1958.5 0.0 copy-done.1
  1958.5 0.0 copy-done.4
  1958.5 0.0 slice-start
  1958.5 0.0 copy-start.3
  1958.5 23.6 %fusion.12 = bf16[256,768]{1,0:T(8,128)(2,1)S(1)} fusion(bf16[768,32768]{1,0:T(8,128)(2,1)} %bitcast.23, bf16[768,32768]{1,0:T(8,128)(2,1)} %all-gather.3.cloned.1.call-done, s32[768]{0:T(1024)S(1)} %copy-done.1, s32[256]{0:T(256)S(1)} %copy-done.4), kind=kOutput, calls=%fused_computation.14 | convolution fusion | flops 12885491712 | bytes 67506176 | tf_op jit(solution)/shard_map/dot_general | solution.py:20
  1982.1 0.0 slice-done
  1982.1 0.0 copy-done.3
  1982.1 0.0 slice-start.1
  1982.1 0.0 copy-start.2
  1982.1 19.0 fusion.18
  2001.1 0.0 slice-done.1
  2001.1 0.0 copy-done.2
  2001.2 15.0 fusion.26
  2016.2 1.1 fusion.22
  (1 shorter events, 0.0 us)
Async XLA Ops:
  6.5 837.8 %all-gather.5.cloned.1.call-start = ((), (), s32[]{:S(2)}) async-start(), calls=%async_computation.2 | async-start | bytes 62914560 | tf_op jit(solution)/shard_map/all_gather | solution.py:38
  7.3 1951.2 %all-gather.3.cloned.1.call-start = ((), (), s32[]{:S(2)}) async-start(), calls=%async_computation.1 | async-start | bytes 62914560 | tf_op jit(solution)/shard_map/all_gather | solution.py:37
  908.8 771.3 %all-to-all-start = ((bf16[3,4,256,8192]{2,3,0,1:T(8,128)(2,1)}), bf16[3,4,256,8192]{2,3,0,1:T(8,128)(2,1)}, u32[]{:S(2)}, u32[]{:S(2)}) async-start(bf16[3,4,256,8192]{2,3,0,1:T(8,128)(2,1)} %copy.10), calls=%async_computation | async-start | bytes 100663296 | tf_op jit(solution)/shard_map/all_to_all | solution.py:40
  920.6 0.6 copy-start
  1916.1 42.4 %copy-start.1 = (s32[768]{0:T(1024)S(1)}, s32[768]{0:T(1024)}, u32[]{:S(2)}) copy-start(s32[768]{0:T(1024)} %copy-done) | copy-start | bytes 9220
  1916.1 42.4 %copy-start.4 = (s32[256]{0:T(256)S(1)}, s32[256]{0:T(256)}, u32[]{:S(2)}) copy-start(s32[256]{0:T(256)} %fusion.44) | copy-start | bytes 3076
  1958.5 23.6 %slice-start = ((s32[768]{0:T(1024)}), s32[512]{0:T(512)S(1)}, s32[]{:S(2)}) async-start(s32[768]{0:T(1024)} %copy-done), calls=%async_computation.3 | async-start | bytes 4096 | tf_op jit(solution)/shard_map/slice | solution.py:23
  1958.5 23.6 %copy-start.3 = (s32[256]{0:T(256)S(1)}, s32[256]{0:T(256)}, u32[]{:S(2)}) copy-start(s32[256]{0:T(256)} %get-tuple-element.6) | copy-start | bytes 3076
  1982.1 19.1 slice-start.1
  1982.1 19.0 copy-start.2
Sparse Core Ops, SparseCore 0:
  8.9 835.3 all-gather.4
  845.9 516.0 all-gather.2
where the time goes:
time: 2030 us; the launch traced here: 2020 us
  waiting for transfers between devices  1600 us (79%)
  local copies, waits for them, and re-layouts  343 us (17%)
  matrix products  57.6 us (3%)
    all_gather x1, waiting for transfers between devices, local_fn(): lax.all_gather(a_local.reshape(local_rows // BLOCK, BLOCK, m_local), 'row...  836 us
    all_to_all x1, waiting for transfers between devices, local_fn(): swapped = lax.all_to_all(grouped, 'col', 1, 3, tiled=True)  758 us
    all_to_all x2, local copies, waits for them, and re-layouts, local_fn(): swapped = lax.all_to_all(grouped, 'col', 1, 3, tiled=True)  115 us
    slice x3, local copies, waits for them, and re-layouts, lower_part(): col_panel[:col_width]  91.5 us
    unnamed x12, local copies, waits for them, and re-layouts  72.1 us
    all_gather x1, local copies, waits for them, and re-layouts, local_fn(): lax.all_gather(a_local.reshape(local_rows // BLOCK, BLOCK, m_local), 'row...  64.5 us
    dot_general x3, matrix products, lower_part(): lax.dot_general(row_panel[first_blk * BLOCK:last_blk * BLOCK], col_panel[...  57.6 us
  transfers between devices with their start and end apart: 3, of which 2 were waited for; matrix products, arithmetic and copies ran while one was open for 17% of the time, Pallas kernels for 0%

commit v1 on v0

v1 whole, which is shorter than its diff:
```python
import jax
import jax.numpy as jnp
from jax import lax
from jax.experimental import pallas as pl
from jax.experimental.pallas import tpu as pltpu
from jax.sharding import PartitionSpec as P

BLOCK = 256
HALF = BLOCK // 2
MESH = pl.DeviceIdType.MESH
STAGES = ((0, BLOCK), (BLOCK, BLOCK), (2 * BLOCK, HALF), (2 * BLOCK + HALF, HALF))
D0, R1, D1, R2A, R2B, D2 = range(6)
DIAG_ROW = {D0: 0, D1: BLOCK, D2: 2 * BLOCK}
SPLIT_ROW = {R2A: 2 * BLOCK, R2B: 2 * BLOCK + HALF}
SELF_TILES = ((0, 0), (1, 0), (2, 0), (1, 1), (2, 1), (2, 2))


def product(left, right):
    return lax.dot_general(left, right, (((1,), (1,)), ((), ())), preferred_element_type=jnp.float32)


def kernel(a_ref, out_ref, panel, chunk, own_part, own_recv, part, core_in, y_in, z1_in, z2_in,
           a_send, a_recv, own_sem, chunk_sem, self_send, self_recv,
           core_send, core_recv, y_send, y_recv, z1_send, z1_recv, z2_send, z2_recv):
    z = lax.axis_index('row')
    col = lax.axis_index('col')
    core = lax.rem(col, 2)
    y = lax.div(col, 2)
    odd = lax.rem(z, 2)
    peers = (z + 1 - 2 * odd, lax.rem(z + 2, 4), 3 - z)
    sibling = {'col': col + 1 - 2 * core}
    y_peer = {'col': lax.rem(col + 2, 4)}
    width = panel.shape[2]
    deep = chunk.shape[2]
    kept = col
    given = lax.rem(col + 2, 4)

    barrier = pltpu.get_barrier_semaphore()
    for dev in (sibling, y_peer, {'row': peers[0]}, {'row': peers[1]}, {'row': peers[2]}):
        pl.semaphore_signal(barrier, inc=1, device_id=dev, device_id_type=MESH)
    pl.semaphore_wait(barrier, 5)

    def remote(src, dst, send, recv, dev):
        return pltpu.make_async_remote_copy(src_ref=src, dst_ref=dst, send_sem=send, recv_sem=recv,
                                            device_id=dev, device_id_type=MESH)

    def a_copy(stage, hop):
        first, count = STAGES[stage]
        peer = peers[hop]
        cols = pl.ds(pl.multiple_of(peer * width, 128), width)
        return remote(a_ref.at[pl.ds(first, count), cols], panel.at[z, pl.ds(first, count)],
                      a_send.at[stage, hop], a_recv.at[stage, hop], {'row': peer})

    def start_sends(order):
        for stage in range(len(STAGES)):
            for hop in order:
                a_copy(stage, hop).start()

    pl.when(core == 0)(lambda: start_sends((1, 2, 0)))
    pl.when(core == 1)(lambda: start_sends((0, 2, 1)))
    own_copy = pltpu.make_async_copy(a_ref.at[:, pl.ds(pl.multiple_of(z * width, 128), width)], panel.at[z], own_sem)
    own_copy.start()

    def chunk_copy(idx, slot):
        cols = pl.ds(pl.multiple_of(idx * deep, 128), deep)
        return pltpu.make_async_copy(a_ref.at[:, cols], chunk.at[slot], chunk_sem.at[slot])

    chunk_copy(0, 0).start()
    out_ref[...] = jnp.zeros_like(out_ref)
    own_part[...] = jnp.zeros_like(own_part)
    chunks = a_ref.shape[1] // deep

    def self_step(idx, carry):
        slot = lax.rem(idx, 2)

        @pl.when(idx + 1 < chunks)
        def _():
            chunk_copy(idx + 1, 1 - slot).start()

        chunk_copy(idx, slot).wait()
        for tile, (up, down) in enumerate(SELF_TILES):
            own_part[tile] += product(chunk[slot, pl.ds(up * BLOCK, BLOCK), :], chunk[slot, pl.ds(down * BLOCK, BLOCK), :])
        return carry

    lax.fori_loop(0, chunks, self_step, 0)
    self_core = remote(own_part, own_recv.at[0], self_send.at[0], self_recv.at[0], sibling)
    self_y = remote(own_part, own_recv.at[1], self_send.at[1], self_recv.at[1], y_peer)
    right_core = core == odd
    right_y = y == lax.div(z, 2)
    pl.when(jnp.logical_not(right_core))(lambda: self_core.start())

    def self_core_add():
        @pl.when(right_core)
        def _():
            self_core.wait_recv()
            own_part[...] += own_recv[0]
            pl.when(jnp.logical_not(right_y))(lambda: self_y.start())

    def self_y_add():
        @pl.when(col == z)
        def _():
            self_y.wait_recv()
            own_part[...] += own_recv[1]
            below = lax.broadcasted_iota(jnp.int32, (BLOCK, BLOCK), 0) >= lax.broadcasted_iota(jnp.int32, (BLOCK, BLOCK), 1)
            for tile, (up, down) in enumerate(SELF_TILES):
                vals = own_part[tile]
                if up == down:
                    vals = jnp.where(below, vals, 0.0)
                out_ref[pl.ds(up * BLOCK, BLOCK), pl.ds(down * BLOCK, BLOCK)] = vals.astype(out_ref.dtype)

    def if_present(flow, c, e, more, act):
        cond = more
        if flow in DIAG_ROW:
            here = c + e + 1 < 4
            cond = here if more is None else jnp.logical_and(more, here)
        if cond is None:
            act()
        else:
            pl.when(cond)(act)

    def core_copy(flow, c, e):
        pair = lax.div(c, 2)
        return remote(part.at[flow, c, e], core_in.at[flow, pair, e], core_send.at[flow, pair, e],
                      core_recv.at[flow, pair, e], sibling)

    def y_copy(flow, e):
        return remote(part.at[flow, given, e], y_in.at[flow, e], y_send.at[flow, e], y_recv.at[flow, e], y_peer)

    def z1_copy(flow, e, r):
        pair = lax.div(r, 2)
        return remote(part.at[flow, kept, e], z1_in.at[flow, pair], z1_send.at[flow, pair], z1_recv.at[flow, pair],
                      {'row': peers[0]})

    def z2_copy(flow, e):
        return remote(part.at[flow, kept, e], z2_in.at[flow], z2_send.at[flow], z2_recv.at[flow], {'row': peers[1]})

    def each(act):
        lax.fori_loop(0, 3, lambda e, carry: (act(e), carry)[1], 0)

    def wait_stage(stage):
        if stage == 0:
            own_copy.wait()
        for hop in range(3):
            a_copy(stage, hop).wait_recv()

    def compute(flow):
        def c_step(c, carry):
            def tile(e):
                r = lax.rem(c + e + 1, 4)

                def act():
                    if flow in DIAG_ROW:
                        rows = pl.ds(DIAG_ROW[flow], BLOCK)
                        part[flow, c, e] = product(panel[r, rows, :], panel[c, rows, :])
                    elif flow in SPLIT_ROW:
                        left = panel[r, pl.ds(SPLIT_ROW[flow], HALF), :]
                        for b in range(2):
                            part[flow, c, e, pl.ds(b * HALF, HALF), :] = product(left, panel[c, pl.ds(b * BLOCK, BLOCK), :])
                    else:
                        part[flow, c, e] = product(panel[r, pl.ds(BLOCK, BLOCK), :], panel[c, pl.ds(0, BLOCK), :])

                if_present(flow, c, e, None, act)

            each(tile)

            @pl.when(lax.rem(c, 2) != core)
            def _():
                each(lambda e: if_present(flow, c, e, None, lambda: core_copy(flow, c, e).start()))

            return carry

        lax.fori_loop(0, 4, c_step, 0)

    def core_add(flow):
        def add_in(c, e):
            core_copy(flow, c, e).wait_recv()
            part[flow, c, e] += core_in[flow, lax.div(c, 2), e]

        def pass_on(e):
            add_in(given, e)
            y_copy(flow, e).start()

        each(lambda e: if_present(flow, given, e, None, lambda: pass_on(e)))
        each(lambda e: if_present(flow, kept, e, None, lambda: add_in(kept, e)))

    def y_add(flow):
        def act(e):
            y_copy(flow, e).wait_recv()
            part[flow, kept, e] += y_in[flow, e]
            r = lax.rem(kept + e + 1, 4)
            pl.when(lax.rem(r, 2) != odd)(lambda: z1_copy(flow, e, r).start())

        each(lambda e: if_present(flow, kept, e, None, lambda: act(e)))

    def z1_add(flow):
        def act(e, r):
            z1_copy(flow, e, r).wait_recv()
            part[flow, kept, e] += z1_in[flow, lax.div(r, 2)]
            pl.when(r != z)(lambda: z2_copy(flow, e).start())

        def step(e):
            r = lax.rem(kept + e + 1, 4)
            if_present(flow, kept, e, lax.rem(r, 2) == odd, lambda: act(e, r))

        each(step)

    def z2_add(flow):
        def act(e):
            z2_copy(flow, e).wait_recv()
            vals = (part[flow, kept, e] + z2_in[flow]).astype(out_ref.dtype)
            if flow in DIAG_ROW:
                out_ref[pl.ds(DIAG_ROW[flow], BLOCK), pl.ds(DIAG_ROW[flow], BLOCK)] = vals
            elif flow in SPLIT_ROW:
                for b in range(2):
                    out_ref[pl.ds(SPLIT_ROW[flow], HALF), pl.ds(b * BLOCK, BLOCK)] = vals[b * HALF:(b + 1) * HALF]
            else:
                out_ref[pl.ds(BLOCK, BLOCK), pl.ds(0, BLOCK)] = vals

        each(lambda e: if_present(flow, kept, e, lax.rem(kept + e + 1, 4) == z, lambda: act(e)))

    def drain(flow):
        for pair in range(2):
            c = 1 - core + 2 * pair
            each(lambda e: if_present(flow, c, e, None, lambda: core_copy(flow, c, e).wait_send()))
        each(lambda e: if_present(flow, given, e, None, lambda: y_copy(flow, e).wait_send()))

        def step(e):
            r = lax.rem(kept + e + 1, 4)
            if_present(flow, kept, e, lax.rem(r, 2) != odd, lambda: z1_copy(flow, e, r).wait_send())
            if_present(flow, kept, e, r == lax.rem(z + 2, 4), lambda: z2_copy(flow, e).wait_send())

        each(step)

    wait_stage(0)
    compute(D0)
    self_core_add()
    core_add(D0)
    wait_stage(1)
    compute(R1)
    compute(D1)
    core_add(R1)
    core_add(D1)
    self_y_add()
    y_add(D0)
    wait_stage(2)
    compute(R2A)
    core_add(R2A)
    y_add(R1)
    y_add(D1)
    y_add(R2A)
    wait_stage(3)
    compute(R2B)
    core_add(R2B)
    compute(D2)
    core_add(D2)
    for flow in (D0, R1, D1, R2A):
        z1_add(flow)
    y_add(R2B)
    y_add(D2)
    z1_add(R2B)
    z1_add(D2)
    for flow in range(6):
        z2_add(flow)

    for stage in range(len(STAGES)):
        for hop in range(3):
            a_copy(stage, hop).wait_send()
    pl.when(jnp.logical_not(right_core))(lambda: self_core.wait_send())
    pl.when(jnp.logical_and(right_core, jnp.logical_not(right_y)))(lambda: self_y.wait_send())
    for flow in range(6):
        drain(flow)


def solution(mesh):
    def local_fn(a_local):
        local_rows, m_local = a_local.shape
        width = m_local // 4
        deep = min(1024, m_local)
        tile = (BLOCK, BLOCK)
        dma = pltpu.SemaphoreType.DMA
        return pl.pallas_call(
            kernel,
            out_shape=jax.ShapeDtypeStruct((local_rows, local_rows), jnp.bfloat16),
            in_specs=[pl.BlockSpec(memory_space=pl.ANY)],
            out_specs=pl.BlockSpec(memory_space=pltpu.VMEM),
            scratch_shapes=[
                pltpu.VMEM((4, local_rows, width), jnp.bfloat16),
                pltpu.VMEM((2, local_rows, deep), jnp.bfloat16),
                pltpu.VMEM((6,) + tile, jnp.float32),
                pltpu.VMEM((2, 6) + tile, jnp.float32),
                pltpu.VMEM((6, 4, 3) + tile, jnp.float32),
                pltpu.VMEM((6, 2, 3) + tile, jnp.float32),
                pltpu.VMEM((6, 3) + tile, jnp.float32),
                pltpu.VMEM((6, 2) + tile, jnp.float32),
                pltpu.VMEM((6,) + tile, jnp.float32),
                dma((4, 3)), dma((4, 3)), dma, dma((2,)), dma((2,)), dma((2,)),
                dma((6, 2, 3)), dma((6, 2, 3)), dma((6, 3)), dma((6, 3)),
                dma((6, 2)), dma((6, 2)), dma((6,)), dma((6,)),
            ],
            compiler_params=pltpu.CompilerParams(collective_id=0, has_side_effects=True, vmem_limit_bytes=67043328),
            name='triangle',
        )(a_local)

    part_spec = P(('batch', 'row'), 'col')
    return jax.shard_map(local_fn, mesh=mesh, in_specs=(part_spec,), out_specs=part_spec, check_vma=False)
```

time: 2030 us -> 370 us (0.18)
  waiting for transfers between devices: 1600 us -> 0 us
  Pallas kernels: 0 us -> 365 us
  local copies, waits for them, and re-layouts: 343 us -> 2.36 us
  matrix products: 57.6 us -> 0 us
    all_gather x2 -> x0, waiting for transfers between devices: 836 us -> none  [the longest x1 836 us: local_fn(): lax.all_gather(a_local.reshape(local_rows // BLOCK, BLOCK, m_local), 'row...]
    all_to_all x1 -> x0, waiting for transfers between devices: 758 us -> none  [local_fn(): swapped = lax.all_to_all(grouped, 'col', 1, 3, tiled=True)]
    pallas_call x0 -> x1, Pallas kernels: none -> 365 us  [local_fn(): pl.pallas_call(kernel, out_shape=jax.ShapeDtypeStruct((local_rows, local_...]
    all_to_all x2 -> x0, local copies, waits for them, and re-layouts: 115 us -> none  [local_fn(): swapped = lax.all_to_all(grouped, 'col', 1, 3, tiled=True)]
    slice x7 -> x0, local copies, waits for them, and re-layouts: 91.5 us -> none  [the longest x3 91.5 us: lower_part(): col_panel[:col_width]]
    unnamed x12 -> x1, local copies, waits for them, and re-layouts: 72.1 us -> 2.36 us
    all_gather x1 -> x0, local copies, waits for them, and re-layouts: 64.5 us -> none  [local_fn(): lax.all_gather(a_local.reshape(local_rows // BLOCK, BLOCK, m_local), 'row...]
    dot_general x3 -> x0, matrix products: 57.6 us -> none  [lower_part(): lax.dot_general(row_panel[first_blk * BLOCK:last_blk * BLOCK], col_panel[...]
  transfers between devices with their start and end apart: 3 -> 0, of which waited for: 2 -> 0; matrix products, arithmetic and copies ran while one was open for 17% -> 0% of each run, Pallas kernels for 0% -> 0%
where the time goes in v1:
time: 370 us; the launch traced here: 368 us
  Pallas kernels  365 us (99%)
    pallas_call x1, Pallas kernels, local_fn(): pl.pallas_call(kernel, out_shape=jax.ShapeDtypeStruct((local_rows, local_...  365 us

profile of v1, /device:TPU:8, one launch (start us, length us, event | category | flops | bytes accessed | tf_op | source)
XLA Modules:
  0.0 367.6 jit_solution(7897523821718226991)
XLA Ops:
  0.0 365.2 %triangle.1 = bf16[768,768]{1,0:T(8,128)(2,1)} custom-call(bf16[768,8192]{1,0:T(8,128)(2,1)} %a_ref.1), custom_call_target="tpu_custom_call" | custom-call | tf_op jit(solution)/shard_map/triangle/pallas_call | solution.py:281
  365.2 2.4 copy.3

commit v2 on v1

--- a/solution.py
+++ b/solution.py
@@ -6,12 +6,14 @@
 from jax.sharding import PartitionSpec as P
 
 BLOCK = 256
-HALF = BLOCK // 2
 MESH = pl.DeviceIdType.MESH
-STAGES = ((0, BLOCK), (BLOCK, BLOCK), (2 * BLOCK, HALF), (2 * BLOCK + HALF, HALF))
-D0, R1, D1, R2A, R2B, D2 = range(6)
+STAGES = ((0, 256), (256, 256), (512, 128), (640, 64), (704, 64))
+FIRST_STAGES = 3
+FLOWS = 7
+D0, R1, D1, R2A, R2B, R2C, D2 = range(FLOWS)
 DIAG_ROW = {D0: 0, D1: BLOCK, D2: 2 * BLOCK}
-SPLIT_ROW = {R2A: 2 * BLOCK, R2B: 2 * BLOCK + HALF}
+SPLIT_ROW = {R2A: (512, 128), R2B: (640, 64), R2C: (704, 64)}
+PLACE = {D0: (0, 0, 256), R1: (1, 0, 256), D1: (2, 0, 256), R2A: (3, 0, 256), R2B: (4, 0, 128), R2C: (4, 128, 128), D2: (5, 0, 256)}
 SELF_TILES = ((0, 0), (1, 0), (2, 0), (1, 1), (2, 1), (2, 2))
 
 
@@ -19,9 +21,10 @@
     return lax.dot_general(left, right, (((1,), (1,)), ((), ())), preferred_element_type=jnp.float32)
 
 
-def kernel(a_ref, out_ref, panel, chunk, own_part, own_recv, part, core_in, y_in, z1_in, z2_in,
+def kernel(a_ref, out_ref, panel, chunk, own_part, own_recv, part, core_in, y_in, z1_in, z2_in, d_z1_in, d_z2_in,
            a_send, a_recv, own_sem, chunk_sem, self_send, self_recv,
-           core_send, core_recv, y_send, y_recv, z1_send, z1_recv, z2_send, z2_recv):
+           core_send, core_recv, y_send, y_recv, z1_send, z1_recv, z2_send, z2_recv,
+           d_z1_send, d_z1_recv, d_z2_send, d_z2_recv):
     z = lax.axis_index('row')
     col = lax.axis_index('col')
     core = lax.rem(col, 2)
@@ -51,13 +54,16 @@
         return remote(a_ref.at[pl.ds(first, count), cols], panel.at[z, pl.ds(first, count)],
                       a_send.at[stage, hop], a_recv.at[stage, hop], {'row': peer})
 
-    def start_sends(order):
-        for stage in range(len(STAGES)):
-            for hop in order:
-                a_copy(stage, hop).start()
-
-    pl.when(core == 0)(lambda: start_sends((1, 2, 0)))
-    pl.when(core == 1)(lambda: start_sends((0, 2, 1)))
+    def start_sends(stages):
+        def in_order(order):
+            for stage in stages:
+                for hop in order:
+                    a_copy(stage, hop).start()
+
+        pl.when(core == 0)(lambda: in_order((1, 2, 0)))
+        pl.when(core == 1)(lambda: in_order((0, 2, 1)))
+
+    start_sends(range(FIRST_STAGES))
     own_copy = pltpu.make_async_copy(a_ref.at[:, pl.ds(pl.multiple_of(z * width, 128), width)], panel.at[z], own_sem)
     own_copy.start()
 
@@ -118,21 +124,25 @@
         else:
             pl.when(cond)(act)
 
+    def view(ref, flow, *idx):
+        slot, first, count = PLACE[flow]
+        return ref.at[(slot,) + idx + (pl.ds(first, count),)]
+
     def core_copy(flow, c, e):
         pair = lax.div(c, 2)
-        return remote(part.at[flow, c, e], core_in.at[flow, pair, e], core_send.at[flow, pair, e],
+        return remote(view(part, flow, c, e), view(core_in, flow, pair, e), core_send.at[flow, pair, e],
                       core_recv.at[flow, pair, e], sibling)
 
     def y_copy(flow, e):
-        return remote(part.at[flow, given, e], y_in.at[flow, e], y_send.at[flow, e], y_recv.at[flow, e], y_peer)
+        return remote(view(part, flow, given, e), view(y_in, flow, e), y_send.at[flow, e], y_recv.at[flow, e], y_peer)
 
     def z1_copy(flow, e, r):
         pair = lax.div(r, 2)
-        return remote(part.at[flow, kept, e], z1_in.at[flow, pair], z1_send.at[flow, pair], z1_recv.at[flow, pair],
+        return remote(view(part, flow, kept, e), view(z1_in, flow, pair), z1_send.at[flow, pair], z1_recv.at[flow, pair],
                       {'row': peers[0]})
 
     def z2_copy(flow, e):
-        return remote(part.at[flow, kept, e], z2_in.at[flow], z2_send.at[flow], z2_recv.at[flow], {'row': peers[1]})
+        return remote(view(part, flow, kept, e), view(z2_in, flow), z2_send.at[flow], z2_recv.at[flow], {'row': peers[1]})
 
     def each(act):
         lax.fori_loop(0, 3, lambda e, carry: (act(e), carry)[1], 0)
@@ -144,6 +154,8 @@
             a_copy(stage, hop).wait_recv()
 
     def compute(flow):
+        slot, first, _ = PLACE[flow]
+
         def c_step(c, carry):
             def tile(e):
                 r = lax.rem(c + e + 1, 4)
@@ -151,13 +163,14 @@
                 def act():
                     if flow in DIAG_ROW:
                         rows = pl.ds(DIAG_ROW[flow], BLOCK)
-                        part[flow, c, e] = product(panel[r, rows, :], panel[c, rows, :])
+                        part[slot, c, e] = product(panel[r, rows, :], panel[c, rows, :])
                     elif flow in SPLIT_ROW:
-                        left = panel[r, pl.ds(SPLIT_ROW[flow], HALF), :]
+                        row, count = SPLIT_ROW[flow]
+                        left = panel[r, pl.ds(row, count), :]
                         for b in range(2):
-                            part[flow, c, e, pl.ds(b * HALF, HALF), :] = product(left, panel[c, pl.ds(b * BLOCK, BLOCK), :])
+                            part[slot, c, e, pl.ds(first + b * count, count), :] = product(left, panel[c, pl.ds(b * BLOCK, BLOCK), :])
                     else:
-                        part[flow, c, e] = product(panel[r, pl.ds(BLOCK, BLOCK), :], panel[c, pl.ds(0, BLOCK), :])
+                        part[slot, c, e] = product(panel[r, pl.ds(BLOCK, BLOCK), :], panel[c, pl.ds(0, BLOCK), :])
 
                 if_present(flow, c, e, None, act)
 
@@ -174,19 +187,22 @@
     def core_add(flow):
         def add_in(c, e):
             core_copy(flow, c, e).wait_recv()
-            part[flow, c, e] += core_in[flow, lax.div(c, 2), e]
+            view(part, flow, c, e)[...] += view(core_in, flow, lax.div(c, 2), e)[...]
 
         def pass_on(e):
             add_in(given, e)
             y_copy(flow, e).start()
 
+        if flow == D2:
+            each_d(lambda pair, c, e, r: (add_in(c, e), pl.when(lax.rem(r, 2) != odd)(lambda: d_z1_copy(pair, c, e, r).start())))
+            return
         each(lambda e: if_present(flow, given, e, None, lambda: pass_on(e)))
         each(lambda e: if_present(flow, kept, e, None, lambda: add_in(kept, e)))
 
     def y_add(flow):
         def act(e):
             y_copy(flow, e).wait_recv()
-            part[flow, kept, e] += y_in[flow, e]
+            view(part, flow, kept, e)[...] += view(y_in, flow, e)[...]
             r = lax.rem(kept + e + 1, 4)
             pl.when(lax.rem(r, 2) != odd)(lambda: z1_copy(flow, e, r).start())
 
@@ -195,7 +211,7 @@
     def z1_add(flow):
         def act(e, r):
             z1_copy(flow, e, r).wait_recv()
-            part[flow, kept, e] += z1_in[flow, lax.div(r, 2)]
+            view(part, flow, kept, e)[...] += view(z1_in, flow, lax.div(r, 2))[...]
             pl.when(r != z)(lambda: z2_copy(flow, e).start())
 
         def step(e):
@@ -207,21 +223,79 @@
     def z2_add(flow):
         def act(e):
             z2_copy(flow, e).wait_recv()
-            vals = (part[flow, kept, e] + z2_in[flow]).astype(out_ref.dtype)
+            vals = (view(part, flow, kept, e)[...] + view(z2_in, flow)[...]).astype(out_ref.dtype)
             if flow in DIAG_ROW:
                 out_ref[pl.ds(DIAG_ROW[flow], BLOCK), pl.ds(DIAG_ROW[flow], BLOCK)] = vals
             elif flow in SPLIT_ROW:
+                row, count = SPLIT_ROW[flow]
                 for b in range(2):
-                    out_ref[pl.ds(SPLIT_ROW[flow], HALF), pl.ds(b * BLOCK, BLOCK)] = vals[b * HALF:(b + 1) * HALF]
+                    out_ref[pl.ds(row, count), pl.ds(b * BLOCK, BLOCK)] = vals[b * count:(b + 1) * count]
             else:
                 out_ref[pl.ds(BLOCK, BLOCK), pl.ds(0, BLOCK)] = vals
 
         each(lambda e: if_present(flow, kept, e, lax.rem(kept + e + 1, 4) == z, lambda: act(e)))
+
+    def each_d(act):
+        for pair in range(2):
+            c = core + 2 * pair
+            each(lambda e: pl.when(c + e + 1 < 4)(lambda: (act(pair, c, e, c + e + 1), None)[1]))
+
+    def d_z1_copy(pair, c, e, r):
+        half = lax.div(r, 2)
+        return remote(part.at[5, c, e], d_z1_in.at[pair, half], d_z1_send.at[pair, half], d_z1_recv.at[pair, half],
+                      {'row': peers[0]})
+
+    def d_z2_copy(pair, c, e):
+        return remote(part.at[5, c, e], d_z2_in.at[pair], d_z2_send.at[pair], d_z2_recv.at[pair], {'row': peers[1]})
+
+    def d_y_copy(c, e):
+        return remote(part.at[5, c, e], y_in.at[5, 0], y_send.at[D2, 0], y_recv.at[D2, 0], y_peer)
+
+    def d_z1_add():
+        def act(pair, c, e, r):
+            @pl.when(lax.rem(r, 2) == odd)
+            def _():
+                d_z1_copy(pair, c, e, r).wait_recv()
+                part[5, c, e] += d_z1_in[pair, lax.div(r, 2)]
+                pl.when(r != z)(lambda: d_z2_copy(pair, c, e).start())
+
+        each_d(act)
+
+    def d_z2_add():
+        def act(pair, c, e, r):
+            @pl.when(r == z)
+            def _():
+                d_z2_copy(pair, c, e).wait_recv()
+                part[5, c, e] += d_z2_in[pair]
+                pl.when(y != pair)(lambda: d_y_copy(c, e).start())
+
+        each_d(act)
+
+    def d_y_add():
+        def act(pair, c, e, r):
+            @pl.when(jnp.logical_and(r == z, y == pair))
+            def _():
+                d_y_copy(c, e).wait_recv()
+                rows = pl.ds(DIAG_ROW[D2], BLOCK)
+                out_ref[rows, rows] = (part[5, c, e] + y_in[5, 0]).astype(out_ref.dtype)
+
+        each_d(act)
+
+    def d_drain():
+        def act(pair, c, e, r):
+            pl.when(lax.rem(r, 2) != odd)(lambda: d_z1_copy(pair, c, e, r).wait_send())
+            pl.when(r == lax.rem(z + 2, 4))(lambda: d_z2_copy(pair, c, e).wait_send())
+            pl.when(jnp.logical_and(r == z, y != pair))(lambda: d_y_copy(c, e).wait_send())
+
+        each_d(act)
 
     def drain(flow):
         for pair in range(2):
             c = 1 - core + 2 * pair
             each(lambda e: if_present(flow, c, e, None, lambda: core_copy(flow, c, e).wait_send()))
+        if flow == D2:
+            d_drain()
+            return
         each(lambda e: if_present(flow, given, e, None, lambda: y_copy(flow, e).wait_send()))
 
         def step(e):
@@ -237,37 +311,50 @@
     core_add(D0)
     wait_stage(1)
     compute(R1)
+    core_add(R1)
     compute(D1)
-    core_add(R1)
     core_add(D1)
     self_y_add()
     y_add(D0)
+    y_add(R1)
+    start_sends(range(FIRST_STAGES, len(STAGES)))
+    y_add(D1)
     wait_stage(2)
     compute(R2A)
     core_add(R2A)
-    y_add(R1)
-    y_add(D1)
+    z1_add(D0)
+    z1_add(R1)
     y_add(R2A)
     wait_stage(3)
     compute(R2B)
     core_add(R2B)
+    y_add(R2B)
+    wait_stage(4)
     compute(D2)
+    compute(R2C)
     core_add(D2)
-    for flow in (D0, R1, D1, R2A):
-        z1_add(flow)
-    y_add(R2B)
-    y_add(D2)
+    core_add(R2C)
+    z1_add(D1)
+    z1_add(R2A)
     z1_add(R2B)
-    z1_add(D2)
-    for flow in range(6):
-        z2_add(flow)
+    d_z1_add()
+    y_add(R2C)
+    z2_add(D0)
+    z2_add(R1)
+    d_z2_add()
+    z1_add(R2C)
+    z2_add(D1)
+    z2_add(R2A)
+    z2_add(R2B)
+    d_y_add()
+    z2_add(R2C)
 
     for stage in range(len(STAGES)):
         for hop in range(3):
             a_copy(stage, hop).wait_send()
     pl.when(jnp.logical_not(right_core))(lambda: self_core.wait_send())
     pl.when(jnp.logical_and(right_core, jnp.logical_not(right_y)))(lambda: self_y.wait_send())
-    for flow in range(6):
+    for flow in range(FLOWS):
         drain(flow)
 
 
@@ -291,11 +378,14 @@
                 pltpu.VMEM((6, 4, 3) + tile, jnp.float32),
                 pltpu.VMEM((6, 2, 3) + tile, jnp.float32),
                 pltpu.VMEM((6, 3) + tile, jnp.float32),
-                pltpu.VMEM((6, 2) + tile, jnp.float32),
-                pltpu.VMEM((6,) + tile, jnp.float32),
-                dma((4, 3)), dma((4, 3)), dma, dma((2,)), dma((2,)), dma((2,)),
-                dma((6, 2, 3)), dma((6, 2, 3)), dma((6, 3)), dma((6, 3)),
-                dma((6, 2)), dma((6, 2)), dma((6,)), dma((6,)),
+                pltpu.VMEM((5, 2) + tile, jnp.float32),
+                pltpu.VMEM((5,) + tile, jnp.float32),
+                pltpu.VMEM((2, 2) + tile, jnp.float32),
+                pltpu.VMEM((2,) + tile, jnp.float32),
+                dma((len(STAGES), 3)), dma((len(STAGES), 3)), dma, dma((2,)), dma((2,)), dma((2,)),
+                dma((FLOWS, 2, 3)), dma((FLOWS, 2, 3)), dma((FLOWS, 3)), dma((FLOWS, 3)),
+                dma((FLOWS, 2)), dma((FLOWS, 2)), dma((FLOWS,)), dma((FLOWS,)),
+                dma((2, 2)), dma((2, 2)), dma((2,)), dma((2,)),
             ],
             compiler_params=pltpu.CompilerParams(collective_id=0, has_side_effects=True, vmem_limit_bytes=67043328),
             name='triangle',

time: 370 us -> 366 us (0.989)
  no operation moved by 1% of the time
where the time goes in v2:
time: 366 us
  Pallas kernels  364 us (99%)
    pallas_call x1, Pallas kernels, local_fn(): pl.pallas_call(kernel, out_shape=jax.ShapeDtypeStruct((local_rows, local_...  364 us

profile of v2, /device:TPU:8, one launch (start us, length us, event | category | flops | bytes accessed | tf_op | source)
XLA Modules:
  0.0 366.2 jit_solution(11311842298063904995)
XLA Ops:
  0.0 363.8 %triangle.1 = bf16[768,768]{1,0:T(8,128)(2,1)} custom-call(bf16[768,8192]{1,0:T(8,128)(2,1)} %a_ref.1), custom_call_target="tpu_custom_call" | custom-call | tf_op jit(solution)/shard_map/triangle/pallas_call | solution.py:368
  363.8 2.4 copy.3

commit v3 on v2

--- a/solution.py
+++ b/solution.py
@@ -54,16 +54,30 @@
         return remote(a_ref.at[pl.ds(first, count), cols], panel.at[z, pl.ds(first, count)],
                       a_send.at[stage, hop], a_recv.at[stage, hop], {'row': peer})
 
-    def start_sends(stages):
+    inner = jnp.logical_or(z == 1, z == 2)
+    outer = jnp.logical_not(inner)
+    every = range(len(STAGES))
+
+    def start_pairs(stages, one, two):
         def in_order(order):
             for stage in stages:
                 for hop in order:
                     a_copy(stage, hop).start()
 
-        pl.when(core == 0)(lambda: in_order((1, 2, 0)))
-        pl.when(core == 1)(lambda: in_order((0, 2, 1)))
-
-    start_sends(range(FIRST_STAGES))
+        pl.when(core == 0)(lambda: in_order((one, two)))
+        pl.when(core == 1)(lambda: in_order((two, one)))
+
+    @pl.when(inner)
+    def _():
+        for stage in every:
+            a_copy(stage, 0).start()
+
+    @pl.when(outer)
+    def _():
+        for stage in every:
+            a_copy(stage, 1).start()
+        start_pairs(every[:FIRST_STAGES], 2, 0)
+
     own_copy = pltpu.make_async_copy(a_ref.at[:, pl.ds(pl.multiple_of(z * width, 128), width)], panel.at[z], own_sem)
     own_copy.start()
 
@@ -94,6 +108,12 @@
     right_core = core == odd
     right_y = y == lax.div(z, 2)
     pl.when(jnp.logical_not(right_core))(lambda: self_core.start())
+
+    @pl.when(inner)
+    def _():
+        for stage in every:
+            a_copy(stage, 0).wait_send()
+        start_pairs(every, 2, 1)
 
     def self_core_add():
         @pl.when(right_core)
@@ -317,7 +337,7 @@
     self_y_add()
     y_add(D0)
     y_add(R1)
-    start_sends(range(FIRST_STAGES, len(STAGES)))
+    pl.when(outer)(lambda: start_pairs(every[FIRST_STAGES:], 2, 0))
     y_add(D1)
     wait_stage(2)
     compute(R2A)
@@ -349,8 +369,9 @@
     d_y_add()
     z2_add(R2C)
 
-    for stage in range(len(STAGES)):
-        for hop in range(3):
+    for stage in every:
+        pl.when(outer)(lambda: a_copy(stage, 0).wait_send())
+        for hop in (1, 2):
             a_copy(stage, hop).wait_send()
     pl.when(jnp.logical_not(right_core))(lambda: self_core.wait_send())
     pl.when(jnp.logical_and(right_core, jnp.logical_not(right_y)))(lambda: self_y.wait_send())

time: 366 us -> 375 us (1.025)
  Pallas kernels: 364 us -> 372 us
    pallas_call x1, Pallas kernels: 364 us -> 372 us  [local_fn(): pl.pallas_call(kernel, out_shape=jax.ShapeDtypeStruct((local_rows, local_...]
where the time goes in v3:
time: 375 us
  Pallas kernels  372 us (99%)
    pallas_call x1, Pallas kernels, local_fn(): pl.pallas_call(kernel, out_shape=jax.ShapeDtypeStruct((local_rows, local_...  372 us

profile of v3, /device:TPU:8, one launch (start us, length us, event | category | flops | bytes accessed | tf_op | source)
XLA Modules:
  0.0 374.8 jit_solution(7000487926958778377)
XLA Ops:
  0.0 372.5 %triangle.1 = bf16[768,768]{1,0:T(8,128)(2,1)} custom-call(bf16[768,8192]{1,0:T(8,128)(2,1)} %a_ref.1), custom_call_target="tpu_custom_call" | custom-call | tf_op jit(solution)/shard_map/triangle/pallas_call | solution.py:389
  372.5 2.4 copy.3

commit v4 on v2

--- a/solution.py
+++ b/solution.py
@@ -21,10 +21,9 @@
     return lax.dot_general(left, right, (((1,), (1,)), ((), ())), preferred_element_type=jnp.float32)
 
 
-def kernel(a_ref, out_ref, panel, chunk, own_part, own_recv, part, core_in, y_in, z1_in, z2_in, d_z1_in, d_z2_in,
+def kernel(a_ref, out_ref, panel, chunk, own_part, own_recv, part, core_in, y_in, z1_in, z2_in,
            a_send, a_recv, own_sem, chunk_sem, self_send, self_recv,
-           core_send, core_recv, y_send, y_recv, z1_send, z1_recv, z2_send, z2_recv,
-           d_z1_send, d_z1_recv, d_z2_send, d_z2_recv):
+           core_send, core_recv, y_send, y_recv, z1_send, z1_recv, z2_send, z2_recv):
     z = lax.axis_index('row')
     col = lax.axis_index('col')
     core = lax.rem(col, 2)
@@ -63,7 +62,9 @@
         pl.when(core == 0)(lambda: in_order((1, 2, 0)))
         pl.when(core == 1)(lambda: in_order((0, 2, 1)))
 
+    inner = jnp.logical_or(z == 1, z == 2)
     start_sends(range(FIRST_STAGES))
+    pl.when(inner)(lambda: start_sends(range(FIRST_STAGES, len(STAGES))))
     own_copy = pltpu.make_async_copy(a_ref.at[:, pl.ds(pl.multiple_of(z * width, 128), width)], panel.at[z], own_sem)
     own_copy.start()
 
@@ -193,9 +194,6 @@
             add_in(given, e)
             y_copy(flow, e).start()
 
-        if flow == D2:
-            each_d(lambda pair, c, e, r: (add_in(c, e), pl.when(lax.rem(r, 2) != odd)(lambda: d_z1_copy(pair, c, e, r).start())))
-            return
         each(lambda e: if_present(flow, given, e, None, lambda: pass_on(e)))
         each(lambda e: if_present(flow, kept, e, None, lambda: add_in(kept, e)))
 
@@ -235,67 +233,10 @@
 
         each(lambda e: if_present(flow, kept, e, lax.rem(kept + e + 1, 4) == z, lambda: act(e)))
 
-    def each_d(act):
-        for pair in range(2):
-            c = core + 2 * pair
-            each(lambda e: pl.when(c + e + 1 < 4)(lambda: (act(pair, c, e, c + e + 1), None)[1]))
-
-    def d_z1_copy(pair, c, e, r):
-        half = lax.div(r, 2)
-        return remote(part.at[5, c, e], d_z1_in.at[pair, half], d_z1_send.at[pair, half], d_z1_recv.at[pair, half],
-                      {'row': peers[0]})
-
-    def d_z2_copy(pair, c, e):
-        return remote(part.at[5, c, e], d_z2_in.at[pair], d_z2_send.at[pair], d_z2_recv.at[pair], {'row': peers[1]})
-
-    def d_y_copy(c, e):
-        return remote(part.at[5, c, e], y_in.at[5, 0], y_send.at[D2, 0], y_recv.at[D2, 0], y_peer)
-
-    def d_z1_add():
-        def act(pair, c, e, r):
-            @pl.when(lax.rem(r, 2) == odd)
-            def _():
-                d_z1_copy(pair, c, e, r).wait_recv()
-                part[5, c, e] += d_z1_in[pair, lax.div(r, 2)]
-                pl.when(r != z)(lambda: d_z2_copy(pair, c, e).start())
-
-        each_d(act)
-
-    def d_z2_add():
-        def act(pair, c, e, r):
-            @pl.when(r == z)
-            def _():
-                d_z2_copy(pair, c, e).wait_recv()
-                part[5, c, e] += d_z2_in[pair]
-                pl.when(y != pair)(lambda: d_y_copy(c, e).start())
-
-        each_d(act)
-
-    def d_y_add():
-        def act(pair, c, e, r):
-            @pl.when(jnp.logical_and(r == z, y == pair))
-            def _():
-                d_y_copy(c, e).wait_recv()
-                rows = pl.ds(DIAG_ROW[D2], BLOCK)
-                out_ref[rows, rows] = (part[5, c, e] + y_in[5, 0]).astype(out_ref.dtype)
-
-        each_d(act)
-
-    def d_drain():
-        def act(pair, c, e, r):
-            pl.when(lax.rem(r, 2) != odd)(lambda: d_z1_copy(pair, c, e, r).wait_send())
-            pl.when(r == lax.rem(z + 2, 4))(lambda: d_z2_copy(pair, c, e).wait_send())
-            pl.when(jnp.logical_and(r == z, y != pair))(lambda: d_y_copy(c, e).wait_send())
-
-        each_d(act)
-
     def drain(flow):
         for pair in range(2):
             c = 1 - core + 2 * pair
             each(lambda e: if_present(flow, c, e, None, lambda: core_copy(flow, c, e).wait_send()))
-        if flow == D2:
-            d_drain()
-            return
         each(lambda e: if_present(flow, given, e, None, lambda: y_copy(flow, e).wait_send()))
 
         def step(e):
@@ -317,13 +258,13 @@
     self_y_add()
     y_add(D0)
     y_add(R1)
-    start_sends(range(FIRST_STAGES, len(STAGES)))
     y_add(D1)
+    z1_add(D0)
+    z1_add(R1)
+    pl.when(jnp.logical_not(inner))(lambda: start_sends(range(FIRST_STAGES, len(STAGES))))
     wait_stage(2)
     compute(R2A)
     core_add(R2A)
-    z1_add(D0)
-    z1_add(R1)
     y_add(R2A)
     wait_stage(3)
     compute(R2B)
@@ -331,23 +272,18 @@
     y_add(R2B)
     wait_stage(4)
     compute(D2)
+    core_add(D2)
     compute(R2C)
-    core_add(D2)
     core_add(R2C)
     z1_add(D1)
     z1_add(R2A)
     z1_add(R2B)
-    d_z1_add()
+    y_add(D2)
     y_add(R2C)
-    z2_add(D0)
-    z2_add(R1)
-    d_z2_add()
+    z1_add(D2)
     z1_add(R2C)
-    z2_add(D1)
-    z2_add(R2A)
-    z2_add(R2B)
-    d_y_add()
-    z2_add(R2C)
+    for flow in (D0, R1, D1, R2A, R2B, D2, R2C):
+        z2_add(flow)
 
     for stage in range(len(STAGES)):
         for hop in range(3):
@@ -378,14 +314,11 @@
                 pltpu.VMEM((6, 4, 3) + tile, jnp.float32),
                 pltpu.VMEM((6, 2, 3) + tile, jnp.float32),
                 pltpu.VMEM((6, 3) + tile, jnp.float32),
-                pltpu.VMEM((5, 2) + tile, jnp.float32),
-                pltpu.VMEM((5,) + tile, jnp.float32),
-                pltpu.VMEM((2, 2) + tile, jnp.float32),
-                pltpu.VMEM((2,) + tile, jnp.float32),
+                pltpu.VMEM((6, 2) + tile, jnp.float32),
+                pltpu.VMEM((6,) + tile, jnp.float32),
                 dma((len(STAGES), 3)), dma((len(STAGES), 3)), dma, dma((2,)), dma((2,)), dma((2,)),
                 dma((FLOWS, 2, 3)), dma((FLOWS, 2, 3)), dma((FLOWS, 3)), dma((FLOWS, 3)),
                 dma((FLOWS, 2)), dma((FLOWS, 2)), dma((FLOWS,)), dma((FLOWS,)),
-                dma((2, 2)), dma((2, 2)), dma((2,)), dma((2,)),
             ],
             compiler_params=pltpu.CompilerParams(collective_id=0, has_side_effects=True, vmem_limit_bytes=67043328),
             name='triangle',

time: 366 us -> 361 us (0.986)
  Pallas kernels: 364 us -> 356 us
    pallas_call x1, Pallas kernels: 364 us -> 356 us  [local_fn(): pl.pallas_call(kernel, out_shape=jax.ShapeDtypeStruct((local_rows, local_...]
where the time goes in v4:
time: 361 us; the launch traced here: 358 us
  Pallas kernels  356 us (99%)
    pallas_call x1, Pallas kernels, local_fn(): pl.pallas_call(kernel, out_shape=jax.ShapeDtypeStruct((local_rows, local_...  356 us

profile of v4, /device:TPU:8, one launch (start us, length us, event | category | flops | bytes accessed | tf_op | source)
XLA Modules:
  0.0 358.3 jit_solution(383653236873892251)
XLA Ops:
  0.0 356.0 %triangle.1 = bf16[768,768]{1,0:T(8,128)(2,1)} custom-call(bf16[768,8192]{1,0:T(8,128)(2,1)} %a_ref.1), custom_call_target="tpu_custom_call" | custom-call | tf_op jit(solution)/shard_map/triangle/pallas_call | solution.py:304
  356.0 2.4 copy.3

commit v5 on v4

--- a/solution.py
+++ b/solution.py
@@ -7,8 +7,7 @@
 
 BLOCK = 256
 MESH = pl.DeviceIdType.MESH
-STAGES = ((0, 256), (256, 256), (512, 128), (640, 64), (704, 64))
-FIRST_STAGES = 3
+STAGES = tuple((row, 64) for row in range(0, 3 * BLOCK, 64))
 FLOWS = 7
 D0, R1, D1, R2A, R2B, R2C, D2 = range(FLOWS)
 DIAG_ROW = {D0: 0, D1: BLOCK, D2: 2 * BLOCK}
@@ -62,9 +61,7 @@
         pl.when(core == 0)(lambda: in_order((1, 2, 0)))
         pl.when(core == 1)(lambda: in_order((0, 2, 1)))
 
-    inner = jnp.logical_or(z == 1, z == 2)
-    start_sends(range(FIRST_STAGES))
-    pl.when(inner)(lambda: start_sends(range(FIRST_STAGES, len(STAGES))))
+    start_sends((0, 1))
     own_copy = pltpu.make_async_copy(a_ref.at[:, pl.ds(pl.multiple_of(z * width, 128), width)], panel.at[z], own_sem)
     own_copy.start()
 
@@ -247,39 +244,55 @@
         each(step)
 
     wait_stage(0)
+    start_sends((2,))
+    self_core_add()
+    wait_stage(1)
+    start_sends((3,))
+    wait_stage(2)
+    start_sends((4,))
+    wait_stage(3)
     compute(D0)
-    self_core_add()
     core_add(D0)
-    wait_stage(1)
+    start_sends((5,))
+    wait_stage(4)
+    start_sends((6,))
+    self_y_add()
+    wait_stage(5)
+    start_sends((7,))
+    wait_stage(6)
+    start_sends((8,))
+    y_add(D0)
+    wait_stage(7)
     compute(R1)
     core_add(R1)
     compute(D1)
     core_add(D1)
-    self_y_add()
-    y_add(D0)
-    y_add(R1)
-    y_add(D1)
+    start_sends((9,))
+    wait_stage(8)
+    start_sends((10,))
     z1_add(D0)
-    z1_add(R1)
-    pl.when(jnp.logical_not(inner))(lambda: start_sends(range(FIRST_STAGES, len(STAGES))))
-    wait_stage(2)
+    wait_stage(9)
     compute(R2A)
     core_add(R2A)
-    y_add(R2A)
-    wait_stage(3)
+    y_add(R1)
+    start_sends((11,))
+    y_add(D1)
+    wait_stage(10)
     compute(R2B)
     core_add(R2B)
-    y_add(R2B)
-    wait_stage(4)
+    z1_add(R1)
+    y_add(R2A)
+    wait_stage(11)
     compute(D2)
     core_add(D2)
     compute(R2C)
     core_add(R2C)
     z1_add(D1)
     z1_add(R2A)
-    z1_add(R2B)
+    y_add(R2B)
     y_add(D2)
     y_add(R2C)
+    z1_add(R2B)
     z1_add(D2)
     z1_add(R2C)
     for flow in (D0, R1, D1, R2A, R2B, D2, R2C):

time: 361 us -> 358 us (level)
  no operation moved by 1% of the time
where the time goes in v5:
time: 358 us
  Pallas kernels  355 us (99%)
    pallas_call x1, Pallas kernels, local_fn(): pl.pallas_call(kernel, out_shape=jax.ShapeDtypeStruct((local_rows, local_...  355 us

profile of v5, /device:TPU:8, one launch (start us, length us, event | category | flops | bytes accessed | tf_op | source)
XLA Modules:
  0.0 357.6 jit_solution(14419418977981475345)
XLA Ops:
  0.0 355.2 %triangle.1 = bf16[768,768]{1,0:T(8,128)(2,1)} custom-call(bf16[768,8192]{1,0:T(8,128)(2,1)} %a_ref.1), custom_call_target="tpu_custom_call" | custom-call | tf_op jit(solution)/shard_map/triangle/pallas_call | solution.py:317
  355.2 2.4 copy.3
